TPU v7x, 32 devices: a whole 2x2x4 slice. The times are simulated.
32 devices in a mesh: grp: 2 (over core), dp: 4 (over z), seq: 4 (over y, x).
Axes of the slice: x: 2, y: 2, z: 4, core: 2. Of those that a mesh axis runs over, the one named last changes fastest.
Arguments:
- latents: bfloat16 [4, 512, 3072], P('dp', 'seq'), may hold values from -6 to 6
- attended: bfloat16 [4, 512, 1536], P('dp', 'seq'), may hold values from -6 to 6
- gating: float32 [4, 3072], P('dp'), may hold values from -4 to 4
- weights: bfloat16 [2, 3072, 1536], P('grp', ('dp', 'seq')), may hold values from -0.15625 to 0.15625
- critic_position: bfloat16 [512, 3072], P('seq'), may hold values from -6 to 6
- critic_gain: float32 [3072], replicated, may hold values from 0.1 to 1.9
- critic_head: float32 [1536], replicated, may hold values from -0.15625 to 0.15625
- token_order: int32 [512], replicated, may hold values from 0 to 511, as said below
Outputs:
- weight_grads: float32 [2, 3072, 1536], P('grp', ('dp', 'seq'))
Inputs may be any that keep to these rules, and one draw needn't show every extreme that they name: token_order is a permutation of the 512 positions; of each aligned block of 128 entries, exactly 32 values fall in each aligned block of 128 values.
All inputs are finite; a program needn't handle non-finite values.
Results may differ from a plain program's by a relative error of at most 0.0029.
Values may be sent and summed in bfloat16 or wider, within the bound.
No kernel may reach another device: no remote copies, remote signals or barrier semaphores. Data moves between devices by JAX's collectives and lax.ppermute only.
A program may use at most 64 MiB of HBM per device.

v0:
```python
from functools import partial
import jax
import jax.numpy as jnp
from jax import lax
from jax.sharding import PartitionSpec as P


def from_behind(block, axis, distance):
    devices = range(lax.axis_size(axis))
    route = [(i - distance, i) for i in devices if i - distance in devices]
    return lax.ppermute(block, axis, route)


def normalize(values, gain):
    factor = lax.rsqrt(jnp.mean(values * values, axis=-1, keepdims=True) + 1e-06)
    return values * factor * gain


def critic_score(hidden, head):
    return jnp.sum(jax.nn.gelu(hidden, approximate=True) * head, axis=-1)


def shards(
    latents, attended, gating, weights, critic_position, critic_gain, critic_head, token_order
):
    length = latents.shape[1]
    model_width = latents.shape[2]
    feature_width = attended.shape[2]
    seq_count = lax.axis_size("seq")
    share_count = length // seq_count
    is_maker = lax.axis_index("grp") == 0
    seq_place = lax.axis_index("seq")
    full_weight = lax.all_gather(weights[0], ("dp", "seq"), axis=0, tiled=True)

    def make_fake():
        projected = jnp.einsum(
            "th,dh->td", attended[0], full_weight, preferred_element_type=jnp.float32
        )
        return (latents[0].astype(jnp.float32) + gating[0][None, :] * projected).astype(
            jnp.bfloat16
        )

    def skip_fake():
        return jnp.zeros((length, model_width), jnp.bfloat16)

    fake_clip = lax.cond(is_maker, make_fake, skip_fake)
    blocks = token_order.reshape(seq_count, length)
    sources = blocks // length
    offsets = jnp.arange(length, dtype=jnp.int32)
    sort_keys = jnp.where(sources == seq_place, offsets[None, :], length + offsets[None, :])
    picked = jnp.argsort(sort_keys, axis=1)[:, :share_count]
    send_rows = (jnp.take_along_axis(blocks, picked, axis=1) - seq_place * length).reshape(-1)
    own_block = lax.dynamic_index_in_dim(blocks, seq_place, 0, keepdims=False)
    own_source = own_block // length
    indicator = (own_source[:, None] == jnp.arange(seq_count, dtype=jnp.int32)[None, :]).astype(
        jnp.int32
    )
    rank_in = jnp.sum(jnp.cumsum(indicator, axis=0) * indicator, axis=1) - 1
    recv_rows = own_source * share_count + rank_in
    outgoing = fake_clip[send_rows].reshape(seq_count, share_count, model_width)
    crossed = from_behind(outgoing, "grp", 1)
    arrived = lax.all_to_all(crossed, "seq", split_axis=0, concat_axis=0, tiled=True)
    critic_tokens = arrived.reshape(length, model_width)[recv_rows]

    def run_critic():
        critic_in = critic_tokens.astype(jnp.float32) + critic_position.astype(jnp.float32)
        normed, norm_back = jax.vjp(partial(normalize, gain=critic_gain), critic_in)
        normed_b = normed.astype(jnp.bfloat16)
        hidden = jnp.dot(normed_b, full_weight, preferred_element_type=jnp.float32)
        scores, score_back = jax.vjp(partial(critic_score, head=critic_head), hidden)
        hidden_grad = score_back(-jax.nn.sigmoid(-scores))[0].astype(jnp.bfloat16)
        normed_grad = jnp.einsum(
            "th,dh->td", hidden_grad, full_weight, preferred_element_type=jnp.float32
        )
        input_grad = norm_back(normed_grad)[0].astype(jnp.bfloat16)
        return (normed_b, hidden_grad, input_grad)

    def skip_critic():
        return (
            jnp.zeros((length, model_width), jnp.bfloat16),
            jnp.zeros((length, feature_width), jnp.bfloat16),
            jnp.zeros((length, model_width), jnp.bfloat16),
        )

    normed_b, hidden_grad, input_grad = lax.cond(jnp.logical_not(is_maker), run_critic, skip_critic)
    returning = input_grad[jnp.argsort(recv_rows)].reshape(seq_count, share_count, model_width)
    regrouped = lax.all_to_all(returning, "seq", split_axis=0, concat_axis=0, tiled=True)
    returned = from_behind(regrouped, "grp", -1)
    fake_grad = returned.reshape(length, model_width)[jnp.argsort(send_rows)]
    projected_grad = (gating[0][None, :] * fake_grad.astype(jnp.float32)).astype(jnp.bfloat16)
    left_side = jnp.where(is_maker, projected_grad, normed_b)
    right_side = jnp.where(is_maker, attended[0], hidden_grad)
    summed = lax.psum_scatter(
        jnp.einsum("td,th->dh", left_side, right_side, preferred_element_type=jnp.float32),
        ("dp", "seq"),
        scatter_dimension=0,
        tiled=True,
    )
    return summed[None]


def solution(mesh):
    return jax.shard_map(
        shards,
        mesh=mesh,
        in_specs=(
            P("dp", "seq", None),
            P("dp", "seq", None),
            P("dp", None),
            P("grp", ("dp", "seq"), None),
            P("seq", None),
            P(),
            P(),
            P(),
        ),
        out_specs=P("grp", ("dp", "seq"), None),
        check_vma=False,
    )
```

profile of v0, /device:TPU:0, one launch (start us, length us, event | category | flops | bytes accessed | tf_op | source)
XLA Modules:
  0.0 489.7 jit_solution(7925361353231627886)
XLA Ops:
  7.4 1.4 iota_select_fusion
  8.8 0.6 iota.26
  9.5 0.5 all-gather.3.cloned.1.call-update
  10.0 3.0 sort.52.cloned.1.call-done
  13.0 0.7 bitcast_or_fusion
  13.8 1.5 gather_fusion.4
  15.5 121.5 %all-gather.3.cloned.1.call-done = bf16[1,3072,1536]{2,1,0:T(8,128)(2,1)} async-done(((bf16[1,192,1536]{2,1,0:T(8,128)(2,1)}), bf16[1,3072,1536]{2,1,0:T(8,128)(2,1)}) %all-gather.3.cloned.1.call-update) | async-done | bytes 9437200 | tf_op jit(solution)/shard_map/all_gather | solution.py:33
  137.0 6.9 %conditional.2 = (bf16[128,3072]{1,0:T(8,128)(2,1)S(1)}) conditional(s32[]{:T(128)} %convert_element_type.45, () %tuple.23, (bf16[1,128,3072]{2,1,0:T(8,128)(2,1)S(1)}, f32[1,3072]{1,0:T(1,128)S(1)}, bf16[1,128,1536]{2,1,0:T(8,128)(2,1)S(1)}, bf16[3072,1536]{1,0:T(8,128)(2,1)}) %tuple.49), branch_computations={%region_0.0_spmd, %region_1.0_spmd} | conditional | flops 1209532416 | bytes 11415560 | solution.py:46
  137.1 6.8 %fusion.1 = bf16[128,3072]{1,0:T(8,128)(2,1)S(1)} fusion(bf16[3072,1536]{1,0:T(8,128)(2,1)} %get-tuple-element.117, bf16[1,128,3072]{2,1,0:T(8,128)(2,1)S(1)} %get-tuple-element.141, f32[3072]{0:T(1024)S(1)} %bitcast.64, bf16[1,128,1536]{2,1,0:T(8,128)(2,1)S(1)} %get-tuple-element.116), kind=kOutput, calls=%fused_computation.7 | convolution fusion | flops 1209532416 | bytes 11415552 | tf_op jit(solution)/shard_map/cond/branch_1_fun/th,dh->td/dot_general | solution.py:36
  143.9 1.0 gather_fusion.1
  144.9 2.3 collective-permute-start
  147.7 0.7 collective-permute-done
  148.4 3.5 all-to-all-start
  152.0 2.5 sort.49
  154.6 9.0 %all-to-all-done = bf16[4,32,3072]{2,1,0:T(8,128)(2,1)S(1)} async-done(((bf16[4,32,3072]{2,1,0:T(8,128)(2,1)}), bf16[4,32,3072]{2,1,0:T(8,128)(2,1)S(1)}, u32[]{:S(2)}, u32[]{:S(2)}) %all-to-all-start) | async-done | bytes 786464 | tf_op jit(solution)/shard_map/all_to_all | solution.py:62
  163.5 0.2 conditional.3
  163.7 1.0 gather_fusion.2
  164.8 11.1 %all_to_all.10 = bf16[4,32,3072]{2,1,0:T(8,128)(2,1)S(1)} all-to-all(bf16[4,32,3072]{2,1,0:T(8,128)(2,1)S(1)} %bitcast.61), channel_id=1, replica_groups=mesh['grp'=2,'dp'=4,'seq'=4] {'seq'}, dimensions={0} | all-to-all | bytes 1572864 | tf_op jit(solution)/shard_map/all_to_all | solution.py:87
  175.8 1.3 collective-permute-start.1
  177.2 2.5 sort.50
  179.8 10.4 %collective-permute-done.1 = bf16[4,32,3072]{2,1,0:T(8,128)(2,1)S(1)} collective-permute-done((bf16[4,32,3072]{2,1,0:T(8,128)(2,1)S(1)}, bf16[4,32,3072]{2,1,0:T(8,128)(2,1)S(1)}, u32[]{:S(2)}, u32[]{:S(2)}) %collective-permute-start.1) | collective-permute-done | bytes 786464 | tf_op jit(solution)/shard_map/ppermute | solution.py:11
  190.2 1.0 gather_fusion.3
  191.2 7.9 %fusion.17 = f32[3072,1536]{1,0:T(8,128)} fusion(bf16[128,3072]{1,0:T(8,128)(2,1)S(1)} %get-tuple-element.138, bf16[128,3072]{1,0:T(8,128)(2,1)S(1)} %gather_fusion.3, f32[3072]{0:T(1024)S(1)} %bitcast.63, pred[]{:T(512)S(6)} %eq.22, bf16[128,1536]{1,0:T(8,128)(2,1)S(1)} %get-tuple-element.139, bf16[1,128,1536]{2,1,0:T(8,128)(2,1)S(1)} %copy-done.7), kind=kOutput, calls=%fused_computation.45 | convolution fusion | flops 1209729024 | bytes 21245952 | tf_op jit(solution)/shard_map/td,th->dh/dot_general | solution.py:94
  199.2 283.1 %reduce-scatter.2.cloned.1.call-done = f32[192,1536]{1,0:T(8,128)} async-done(((f32[3072,1536]{1,0:T(8,128)}), f32[192,1536]{1,0:T(8,128)}) %reduce-scatter.2.cloned.1.call-update) | async-done | bytes 1179664 | tf_op jit(solution)/shard_map/reduce_scatter | solution.py:93
  (46 shorter events, 1.2 us)
Async XLA Ops:
  7.4 6.4 %copy-start = (s32[512]{0:T(512)S(1)}, s32[512]{0:T(512)}, u32[]{:S(2)}) copy-start(s32[512]{0:T(512)} %param.19) | copy-start | bytes 6148
  7.4 129.6 %copy-start.9 = (f32[1,3072]{1,0:T(1,128)S(1)}, f32[1,3072]{1,0:T(1,128)}, u32[]{:S(2)}) copy-start(f32[1,3072]{1,0:T(1,128)} %param.14) | copy-start | bytes 36868
  7.4 129.6 %copy-start.6 = (bf16[1,128,1536]{2,1,0:T(8,128)(2,1)S(1)}, bf16[1,128,1536]{2,1,0:T(8,128)(2,1)}, u32[]{:S(2)}) copy-start(bf16[1,128,1536]{2,1,0:T(8,128)(2,1)} %param.13) | copy-start | bytes 1179652
  7.4 129.6 %copy-start.8 = (bf16[1,128,3072]{2,1,0:T(8,128)(2,1)S(1)}, bf16[1,128,3072]{2,1,0:T(8,128)(2,1)}, u32[]{:S(2)}) copy-start(bf16[1,128,3072]{2,1,0:T(8,128)(2,1)} %param.12) | copy-start | bytes 2359300
  7.4 5.6 %sort.52.cloned.1.call-start = ((), (), s32[]{:S(2)}) async-start(), calls=%async_computation.5 | async-start | bytes 12320 | tf_op jit(solution)/shard_map/jit(argsort)/sort | solution.py:51
  9.4 127.6 %all-gather.3.cloned.1.call-start = ((), (), s32[]{:S(2)}) async-start(), calls=%async_computation.4 | async-start | bytes 10027008 | tf_op jit(solution)/shard_map/all_gather | solution.py:33
  13.0 2.4 copy-start.14
  15.4 121.6 %copy-start.11 = (s32[4,32]{1,0:T(4,128)}, s32[4,32]{1,0:T(4,128)S(1)}, u32[]{:S(2)}) copy-start(s32[4,32]{1,0:T(4,128)S(1)} %select_subtract_fusion) | copy-start | bytes 1540
  144.9 18.6 %copy-start.1 = (bf16[128,3072]{1,0:T(8,128)(2,1)S(1)}, bf16[128,3072]{1,0:T(8,128)(2,1)}, u32[]{:S(2)}) copy-start(bf16[128,3072]{1,0:T(8,128)(2,1)} %param.16) | copy-start | bytes 2359300
  144.9 3.5 collective-permute-start
  148.4 15.1 %all-to-all-start = ((bf16[4,32,3072]{2,1,0:T(8,128)(2,1)}), bf16[4,32,3072]{2,1,0:T(8,128)(2,1)S(1)}, u32[]{:S(2)}, u32[]{:S(2)}) async-start(bf16[4,32,3072]{2,1,0:T(8,128)(2,1)} %collective-permute-done), calls=%async_computation | async-start | bytes 1572864 | tf_op jit(solution)/shard_map/all_to_all | solution.py:62
  151.9 330.4 %reduce-scatter.2.cloned.1.call-start = ((), (), s32[]{:S(2)}) async-start(), calls=%async_computation.3 | async-start | bytes 20054016 | tf_op jit(solution)/shard_map/reduce_scatter | solution.py:93
  164.8 12.4 %copy-start.12 = (s32[4,32]{1,0:T(4,128)S(1)}, s32[4,32]{1,0:T(4,128)}, u32[]{:S(2)}) copy-start(s32[4,32]{1,0:T(4,128)} %copy-done.11) | copy-start | bytes 1540
  175.8 14.3 %collective-permute-start.1 = (bf16[4,32,3072]{2,1,0:T(8,128)(2,1)S(1)}, bf16[4,32,3072]{2,1,0:T(8,128)(2,1)S(1)}, u32[]{:S(2)}, u32[]{:S(2)}) collective-permute-start(bf16[4,32,3072]{2,1,0:T(8,128)(2,1)S(1)} %all_to_all.10), channel_id=1, source_target_pairs={{16,0},{17,1},{18,2},{19,3},{20,4},{21,5},{22,6},{23,7},{24,8},{25... | collective-permute-start | bytes 2359304 | tf_op jit(solution)/shard_map/ppermute | solution.py:11
  190.2 1.0 copy-start.7
Sparse Core Ops, SparseCore 0:
  10.4 2.2 sort.54.cloned.1.call-done
  (1 shorter events, 0.0 us)
Sparse Core Ops, SparseCore 1:
  12.7 124.3 all-gather.2
  199.2 283.0 reduce-scatter.1
where the time goes:
time: 490 us
  waiting for transfers between devices  425 us (87%)
  between operations  15 us (3%)
  matrix products  14.7 us (3%)
  blocking collectives  11.1 us (2%)
  local copies, waits for them, and re-layouts  8.77 us (2%)
  other arithmetic  7.69 us (2%)
  starting transfers between devices  7.17 us (1%)
    reduce_scatter x1, waiting for transfers between devices, shards(): lax.psum_scatter(jnp.einsum('td,th->dh', left_side, right_side, preferred...  283 us
    all_gather x1, waiting for transfers between devices, shards(): full_weight = lax.all_gather(weights[0], ('dp', 'seq'), axis=0, tiled=True)  121 us
    ppermute x2, waiting for transfers between devices, from_behind(): return lax.ppermute(block, axis, route)  11.1 us
    all_to_all x1, blocking collectives, shards(): lax.all_to_all(returning, 'seq', split_axis=0, concat_axis=0, tiled=True)  11.1 us
  transfers between devices with their start and end apart: 5, of which 5 were waited for; matrix products, arithmetic and copies ran while one was open for 2% of the time, Pallas kernels for 0%

commit v1 on v0

--- a/solution.py
+++ b/solution.py
@@ -30,7 +30,11 @@
     share_count = length // seq_count
     is_maker = lax.axis_index("grp") == 0
     seq_place = lax.axis_index("seq")
-    full_weight = lax.all_gather(weights[0], ("dp", "seq"), axis=0, tiled=True)
+    own = weights[0]
+    peers = lax.axis_size(("dp", "seq"))
+    pieces = jnp.stack([own for _ in range(peers)])
+    pieces = lax.all_to_all(pieces, ("dp", "seq"), split_axis=0, concat_axis=0)
+    full_weight = jnp.concatenate(pieces, axis=0)
 
     def make_fake():
         projected = jnp.einsum(

time: 490 us -> 594 us (1.21)
  waiting for transfers between devices: 425 us -> 503 us
  starting transfers between devices: 7.17 us -> 27 us
  local copies, waits for them, and re-layouts: 8.77 us -> 15.9 us
    all_to_all x0 -> x1, waiting for transfers between devices: none -> 170 us  [shards(): pieces = lax.all_to_all(pieces, ('dp', 'seq'), split_axis=0, concat_axis=0)]
    all_gather x1 -> x0, waiting for transfers between devices: 121 us -> none  [shards(): full_weight = lax.all_gather(weights[0], ('dp', 'seq'), axis=0, tiled=True)]
    reduce_scatter x1, waiting for transfers between devices: 283 us -> 310 us  [shards(): lax.psum_scatter(jnp.einsum('td,th->dh', left_side, right_side, preferred...]
    all_to_all x1, starting transfers between devices: 3.49 us -> 14.9 us  [shards(): lax.all_to_all(crossed, 'seq', split_axis=0, concat_axis=0, tiled=True)]
    all_to_all x0 -> x1, starting transfers between devices: none -> 8.52 us  [shards(): pieces = lax.all_to_all(pieces, ('dp', 'seq'), split_axis=0, concat_axis=0)]
where the time goes in v1:
time: 594 us; the launch traced here: 593 us
  waiting for transfers between devices  503 us (85%)
  starting transfers between devices  27 us (5%)
  local copies, waits for them, and re-layouts  15.9 us (3%)
  matrix products  14.8 us (2%)
  between operations  13.6 us (2%)
  blocking collectives  11 us (2%)
  other arithmetic  7.51 us (1%)
    reduce_scatter x1, waiting for transfers between devices, shards(): lax.psum_scatter(jnp.einsum('td,th->dh', left_side, right_side, preferred...  310 us
    all_to_all x1, waiting for transfers between devices, shards(): pieces = lax.all_to_all(pieces, ('dp', 'seq'), split_axis=0, concat_axis=0)  170 us
    all_to_all x1, starting transfers between devices, shards(): lax.all_to_all(crossed, 'seq', split_axis=0, concat_axis=0, tiled=True)  14.9 us
    ppermute x2, waiting for transfers between devices, from_behind(): return lax.ppermute(block, axis, route)  14.7 us
  transfers between devices with their start and end apart: 5, of which 5 were waited for; matrix products, arithmetic and copies ran while one was open for 2% of the time, Pallas kernels for 0%

profile of v1, /device:TPU:0, one launch (start us, length us, event | category | flops | bytes accessed | tf_op | source)
XLA Modules:
  0.0 593.0 jit_solution(13529353357310603598)
XLA Ops:
  6.5 5.6 stack.3
  12.2 8.5 %all-to-all-start = ((bf16[16,192,1536]{2,1,0:T(8,128)(2,1)}), bf16[16,192,1536]{2,1,0:T(8,128)(2,1)}, u32[]{:S(2)}, u32[]{:S(2)}) async-start(bf16[16,192,1536]{2,1,0:T(8,128)(2,1)} %stack.3), calls=%async_computation | async-start | bytes 18874368 | tf_op jit(solution)/shard_map/all_to_all | solution.py:36
  20.8 0.6 iota_select_fusion
  22.0 4.3 sort.52.cloned.1.call-done
  26.4 0.8 bitcast_or_fusion
  27.2 1.5 gather_fusion.4
  28.9 169.7 %all-to-all-done = bf16[16,192,1536]{2,1,0:T(8,128)(2,1)} async-done(((bf16[16,192,1536]{2,1,0:T(8,128)(2,1)}), bf16[16,192,1536]{2,1,0:T(8,128)(2,1)}, u32[]{:S(2)}, u32[]{:S(2)}) %all-to-all-start) | async-done | bytes 9437216 | tf_op jit(solution)/shard_map/all_to_all | solution.py:36
  198.7 6.9 %conditional.2 = (bf16[128,3072]{1,0:T(8,128)(2,1)S(1)}) conditional(s32[]{:T(128)} %convert_element_type.45, () %tuple.23, (bf16[1,128,3072]{2,1,0:T(8,128)(2,1)S(1)}, f32[1,3072]{1,0:T(1,128)S(1)}, bf16[1,128,1536]{2,1,0:T(8,128)(2,1)S(1)}, bf16[3072,1536]{1,0:T(8,128)(2,1)}) %tuple.45), branch_computations={%region_0.0_spmd, %region_1.0_spmd} | conditional | flops 1209532416 | bytes 11415560 | solution.py:50
  198.7 6.8 %fusion.1 = bf16[128,3072]{1,0:T(8,128)(2,1)S(1)} fusion(bf16[3072,1536]{1,0:T(8,128)(2,1)} %get-tuple-element.117, bf16[1,128,3072]{2,1,0:T(8,128)(2,1)S(1)} %get-tuple-element.141, f32[3072]{0:T(1024)S(1)} %bitcast.62, bf16[1,128,1536]{2,1,0:T(8,128)(2,1)S(1)} %get-tuple-element.116), kind=kOutput, calls=%fused_computation.7 | convolution fusion | flops 1209532416 | bytes 11415552 | tf_op jit(solution)/shard_map/cond/branch_1_fun/th,dh->td/dot_general | solution.py:40
  205.5 1.0 gather_fusion.1
  206.6 2.3 collective-permute-start
  209.4 0.7 collective-permute-done
  210.1 14.9 %all-to-all-start.1 = ((bf16[4,32,3072]{2,1,0:T(8,128)(2,1)}), bf16[4,32,3072]{2,1,0:T(8,128)(2,1)S(1)}, u32[]{:S(2)}, u32[]{:S(2)}) async-start(bf16[4,32,3072]{2,1,0:T(8,128)(2,1)} %collective-permute-done), calls=%async_computation.1 | async-start | bytes 1572864 | tf_op jit(solution)/shard_map/all_to_all | solution.py:66
  224.9 2.5 sort.49
  227.5 0.6 pad_clamp_fusion.2
  228.1 8.5 %all-to-all-done.1 = bf16[4,32,3072]{2,1,0:T(8,128)(2,1)S(1)} async-done(((bf16[4,32,3072]{2,1,0:T(8,128)(2,1)}), bf16[4,32,3072]{2,1,0:T(8,128)(2,1)S(1)}, u32[]{:S(2)}, u32[]{:S(2)}) %all-to-all-start.1) | async-done | bytes 786464 | tf_op jit(solution)/shard_map/all_to_all | solution.py:66
  236.7 1.2 gather_fusion.2
  237.9 11.0 %all_to_all.15 = bf16[4,32,3072]{2,1,0:T(8,128)(2,1)S(1)} all-to-all(bf16[4,32,3072]{2,1,0:T(8,128)(2,1)S(1)} %bitcast.58), channel_id=1, replica_groups=mesh['grp'=2,'dp'=4,'seq'=4] {'seq'}, dimensions={0} | all-to-all | bytes 1572864 | tf_op jit(solution)/shard_map/all_to_all | solution.py:91
  249.0 1.3 collective-permute-start.1
  250.4 2.5 sort.50
  252.9 14.1 %collective-permute-done.1 = bf16[4,32,3072]{2,1,0:T(8,128)(2,1)S(1)} collective-permute-done((bf16[4,32,3072]{2,1,0:T(8,128)(2,1)S(1)}, bf16[4,32,3072]{2,1,0:T(8,128)(2,1)S(1)}, u32[]{:S(2)}, u32[]{:S(2)}) %collective-permute-start.1) | collective-permute-done | bytes 786464 | tf_op jit(solution)/shard_map/ppermute | solution.py:11
  267.0 1.0 gather_fusion.3
  268.0 7.9 %fusion.17 = f32[3072,1536]{1,0:T(8,128)} fusion(bf16[128,3072]{1,0:T(8,128)(2,1)S(1)} %get-tuple-element.138, bf16[128,3072]{1,0:T(8,128)(2,1)S(1)} %gather_fusion.3, f32[3072]{0:T(1024)S(1)} %bitcast.61, pred[]{:T(512)S(6)} %eq.22, bf16[128,1536]{1,0:T(8,128)(2,1)S(1)} %get-tuple-element.139, bf16[1,128,1536]{2,1,0:T(8,128)(2,1)S(1)} %copy-done.7), kind=kOutput, calls=%fused_computation.45 | convolution fusion | flops 1209729024 | bytes 21245952 | tf_op jit(solution)/shard_map/td,th->dh/dot_general | solution.py:98
  276.0 310.2 %reduce-scatter.2.cloned.1.call-done = f32[192,1536]{1,0:T(8,128)} async-done(((f32[3072,1536]{1,0:T(8,128)}), f32[192,1536]{1,0:T(8,128)}) %reduce-scatter.2.cloned.1.call-update) | async-done | bytes 1179664 | tf_op jit(solution)/shard_map/reduce_scatter | solution.py:97
  (46 shorter events, 1.9 us)
Async XLA Ops:
  12.2 8.6 %copy-start = (s32[512]{0:T(512)S(1)}, s32[512]{0:T(512)}, u32[]{:S(2)}) copy-start(s32[512]{0:T(512)} %param.19) | copy-start | bytes 6148
  12.2 186.5 %all-to-all-start = ((bf16[16,192,1536]{2,1,0:T(8,128)(2,1)}), bf16[16,192,1536]{2,1,0:T(8,128)(2,1)}, u32[]{:S(2)}, u32[]{:S(2)}) async-start(bf16[16,192,1536]{2,1,0:T(8,128)(2,1)} %stack.3), calls=%async_computation | async-start | bytes 18874368 | tf_op jit(solution)/shard_map/all_to_all | solution.py:36
  20.7 178.0 %copy-start.6 = (bf16[1,128,1536]{2,1,0:T(8,128)(2,1)S(1)}, bf16[1,128,1536]{2,1,0:T(8,128)(2,1)}, u32[]{:S(2)}) copy-start(bf16[1,128,1536]{2,1,0:T(8,128)(2,1)} %param.13) | copy-start | bytes 1179652
  20.7 177.9 %copy-start.8 = (bf16[1,128,3072]{2,1,0:T(8,128)(2,1)S(1)}, bf16[1,128,3072]{2,1,0:T(8,128)(2,1)}, u32[]{:S(2)}) copy-start(bf16[1,128,3072]{2,1,0:T(8,128)(2,1)} %param.12) | copy-start | bytes 2359300
  20.7 177.9 %copy-start.9 = (f32[1,3072]{1,0:T(1,128)S(1)}, f32[1,3072]{1,0:T(1,128)}, u32[]{:S(2)}) copy-start(f32[1,3072]{1,0:T(1,128)} %param.14) | copy-start | bytes 36868
  20.7 5.6 sort.52.cloned.1.call-start
  26.4 2.4 copy-start.14
  28.8 169.9 %copy-start.11 = (s32[4,32]{1,0:T(4,128)}, s32[4,32]{1,0:T(4,128)S(1)}, u32[]{:S(2)}) copy-start(s32[4,32]{1,0:T(4,128)S(1)} %select_subtract_fusion) | copy-start | bytes 1540
  206.6 30.0 %copy-start.1 = (bf16[128,3072]{1,0:T(8,128)(2,1)S(1)}, bf16[128,3072]{1,0:T(8,128)(2,1)}, u32[]{:S(2)}) copy-start(bf16[128,3072]{1,0:T(8,128)(2,1)} %param.16) | copy-start | bytes 2359300
  206.6 3.5 collective-permute-start
  210.1 26.5 %all-to-all-start.1 = ((bf16[4,32,3072]{2,1,0:T(8,128)(2,1)}), bf16[4,32,3072]{2,1,0:T(8,128)(2,1)S(1)}, u32[]{:S(2)}, u32[]{:S(2)}) async-start(bf16[4,32,3072]{2,1,0:T(8,128)(2,1)} %collective-permute-done), calls=%async_computation.1 | async-start | bytes 1572864 | tf_op jit(solution)/shard_map/all_to_all | solution.py:66
  224.9 361.3 %reduce-scatter.2.cloned.1.call-start = ((), (), s32[]{:S(2)}) async-start(), calls=%async_computation.4 | async-start | bytes 20054016 | tf_op jit(solution)/shard_map/reduce_scatter | solution.py:97
  237.9 12.3 %copy-start.12 = (s32[4,32]{1,0:T(4,128)S(1)}, s32[4,32]{1,0:T(4,128)}, u32[]{:S(2)}) copy-start(s32[4,32]{1,0:T(4,128)} %copy-done.11) | copy-start | bytes 1540
  249.0 18.0 %collective-permute-start.1 = (bf16[4,32,3072]{2,1,0:T(8,128)(2,1)S(1)}, bf16[4,32,3072]{2,1,0:T(8,128)(2,1)S(1)}, u32[]{:S(2)}, u32[]{:S(2)}) collective-permute-start(bf16[4,32,3072]{2,1,0:T(8,128)(2,1)S(1)} %all_to_all.15), channel_id=1, source_target_pairs={{16,0},{17,1},{18,2},{19,3},{20,4},{21,5},{22,6},{23,7},{24,8},{25... | collective-permute-start | bytes 2359304 | tf_op jit(solution)/shard_map/ppermute | solution.py:11
  267.0 1.0 copy-start.7
Sparse Core Ops, SparseCore 0:
  23.8 2.2 sort.54.cloned.1.call-done
  276.1 310.0 reduce-scatter.1
  (1 shorter events, 0.0 us)
